TPU v7x, 256 devices: a whole 4x4x8 slice. The times are simulated.
256 devices in a mesh: row: 32 (over z, x_lo, core), col: 8 (over x_hi, y).
Axes of the slice: x: 4 (x_hi: 2, x_lo: 2; x = x_hi * 2 + x_lo), y: 4, z: 8, core: 2. Of those that a mesh axis runs over, the one named last changes fastest.
Arguments:
- pair_map: float32 [512, 512, 128], P('row', 'col'), may hold values from -6 to 6
- pair_mask: int32 [512, 512], P('row', 'col'), may hold values 0 or 1
- in_gain: float32 [128], replicated, may hold values from 0.25 to 1.75
- in_bias: float32 [128], replicated, may hold values from -3 to 3
- w_proj: bfloat16 [128, 512], replicated, may hold values from -0.5 to 0.5
- w_gate: bfloat16 [128, 128], replicated, may hold values from -0.5 to 0.5
- out_gain: float32 [128], replicated, may hold values from 0.25 to 1.75
- out_bias: float32 [128], replicated, may hold values from -3 to 3
- w_out: bfloat16 [128, 128], replicated, may hold values from -0.5 to 0.5
Outputs:
- update: float32 [512, 512, 128], P('row', 'col')
All inputs are finite; a program needn't handle non-finite values. No bound on the sum of `pair_mask` on one device may be relied on, other than what follows from the above.
Results may differ from a plain program's by a relative error of at most 0.0035.
Values may be sent and summed in bfloat16 or wider, within the bound.
A program may use at most 128 MiB of HBM per device.

v0:
```python
import jax
import jax.numpy as jnp
from jax import lax
from jax.sharding import Mesh
from jax.sharding import PartitionSpec as P

COL = ("col_0", "col_1")


def own_block(blocks, axes, sequence):
    inside = blocks.shape[1:]
    blocks = blocks.reshape(*(lax.axis_size(a) for a in axes), *inside)
    blocks = jnp.moveaxis(blocks, sequence, range(len(axes))).reshape(-1, *inside)
    for k in sequence:
        blocks = lax.psum_scatter(blocks, axes[k], scatter_dimension=0, tiled=True)
    return blocks[0]


def cut_along(x, dim, count):
    shape = x.shape
    blocks = x.reshape(*shape[:dim], count, shape[dim] // count, *shape[dim + 1 :])
    return jnp.moveaxis(blocks, dim, 0)


def sum_by_axis(x, axes, sequence, dim):
    count = lax.axis_size(axes)
    return own_block(cut_along(x, dim, count), axes, sequence)


def layer_norm(values, gain, bias):
    average = jnp.mean(values, axis=-1, keepdims=True)
    variance = jnp.mean(jnp.square(values - average), axis=-1, keepdims=True)
    return (values - average) * lax.rsqrt(variance + 1e-05) * gain + bias


def local(pair_map, pair_mask, in_gain, in_bias, w_proj, w_gate, out_gain, out_bias, w_out):
    row_count, col_count, channels = pair_map.shape
    hidden_width = w_out.shape[0]
    normed_map = layer_norm(pair_map, in_gain, in_bias).astype(jnp.bfloat16)
    flattened = normed_map.reshape(-1, channels)
    projected_all = jnp.dot(flattened, w_proj, preferred_element_type=jnp.float32).reshape(
        row_count, col_count, 4 * hidden_width
    )
    masked = pair_mask.astype(jnp.float32)[..., None]
    left_side = (
        masked
        * jax.nn.sigmoid(projected_all[..., :hidden_width])
        * projected_all[..., hidden_width : 2 * hidden_width]
    ).astype(jnp.bfloat16)
    gating = jax.nn.sigmoid(jnp.dot(flattened, w_gate, preferred_element_type=jnp.float32)).reshape(
        row_count, col_count, channels
    )
    right_side = (
        masked
        * jax.nn.sigmoid(projected_all[..., 2 * hidden_width : 3 * hidden_width])
        * projected_all[..., 3 * hidden_width :]
    ).astype(jnp.bfloat16)
    partial_value = jnp.einsum(
        "ikc,jkc->ijc",
        left_side,
        lax.all_gather(right_side, "row", axis=0, tiled=True),
        preferred_element_type=jnp.float32,
    )
    summed = sum_by_axis(partial_value, COL, (1, 0), 1)
    normed_sum = layer_norm(summed, out_gain, out_bias).astype(jnp.bfloat16)
    result = jnp.dot(
        normed_sum.reshape(-1, hidden_width), w_out, preferred_element_type=jnp.float32
    ).reshape(row_count, col_count, channels)
    return gating * result


def solution(mesh):
    split = Mesh(mesh.devices.reshape(mesh.shape["row"], 2, 4), ("row", "col_0", "col_1"))
    placed = (P("row", COL, None), P("row", COL), P(), P(), P(), P(), P(), P(), P())
    return jax.shard_map(
        local, mesh=split, in_specs=placed, out_specs=P("row", COL, None), check_vma=False
    )
```

profile of v0, /device:TPU:17, one launch (start us, length us, event | category | flops | bytes accessed | tf_op | source)
XLA Modules:
  0.0 220.1 jit_solution(14188799193320763194)
XLA Ops:
  6.5 0.0 copy-start
  6.5 0.0 all-gather.2.cloned.1.call-start
  6.5 1.3 reduce_sum.36
  7.8 1.4 multiply_reduce_fusion.1
  9.3 0.7 convert_element_type.18
  10.0 1.4 add_convert_fusion.1
  11.4 0.0 copy-done
  11.4 0.4 fusion.17
  11.8 1.0 fusion.3
  12.8 0.0 all-gather.2.cloned.1.call-update
  12.9 0.0 reduce-scatter.3.cloned.1.call-start
  12.9 0.4 copy.18
  13.4 74.5 %all-gather.2.cloned.1.call-done = bf16[512,64,128]{2,1,0:T(8,128)(2,1)} async-done(((bf16[16,64,128]{2,1,0:T(8,128)(2,1)}), bf16[512,64,128]{2,1,0:T(8,128)(2,1)}) %all-gather.2.cloned.1.call-update) | async-done | bytes 8388624 | tf_op jit(solution)/shard_map/all_gather | solution.py:61
  87.8 23.7 %copy.17 = bf16[512,64,128]{1,0,2:T(8,128)(2,1)} copy(bf16[512,64,128]{2,1,0:T(8,128)(2,1)} %all-gather.2.cloned.1.call-done) | data formatting | bytes 16777216 | tf_op jit(solution)/shard_map/all_gather | solution.py:61
  111.5 9.4 %convolution_bitcast_fusion = f32[16,512,128]{1,0,2:T(8,128)} fusion(bf16[512,64,128]{1,0,2:T(8,128)(2,1)} %copy.17, bf16[16,64,128]{1,0,2:T(8,128)(2,1)S(1)} %copy.18), kind=kOutput, calls=%fused_computation | convolution fusion | flops 134217728 | bytes 12845056 | tf_op jit(solution)/shard_map/ikc,jkc->ijc/dot_general | solution.py:58
  120.9 5.3 %copy.19 = f32[16,512,128]{2,1,0:T(8,128)} copy(f32[16,512,128]{1,0,2:T(8,128)} %convolution_bitcast_fusion) | data formatting | bytes 8388608 | tf_op jit(solution)/shard_map/ikc,jkc->ijc/transpose | solution.py:58
  126.2 4.7 %copy.20 = f32[4,2,16,64,128]{4,3,2,1,0:T(8,128)} copy(f32[4,2,16,64,128]{4,3,0,1,2:T(8,128)} %bitcast.31) | data formatting | bytes 8388608 | tf_op jit(solution)/shard_map/transpose | solution.py:13
  130.9 0.0 copy-start.4
  130.9 0.0 copy-start.1
  130.9 0.0 reduce-scatter.3.cloned.1.call-update
  131.0 0.0 reduce-scatter.5.cloned.1.call-start
  131.0 46.8 %reduce-scatter.3.cloned.1.call-done = f32[2,16,64,128]{3,2,1,0:T(8,128)} async-done(((f32[8,16,64,128]{3,2,1,0:T(8,128)}), f32[2,16,64,128]{3,2,1,0:T(8,128)}) %reduce-scatter.3.cloned.1.call-update) | async-done | bytes 1048592 | tf_op jit(solution)/shard_map/reduce_scatter | solution.py:15
  177.9 0.0 reduce-scatter.5.cloned.1.call-update
  177.9 0.0 copy-done.4
  177.9 0.3 fusion.2
  178.2 30.4 %reduce-scatter.5.cloned.1.call-done = f32[1,16,64,128]{3,2,1,0:T(8,128)} async-done(((f32[2,16,64,128]{3,2,1,0:T(8,128)}), f32[1,16,64,128]{3,2,1,0:T(8,128)}) %reduce-scatter.5.cloned.1.call-update) | async-done | bytes 524304 | tf_op jit(solution)/shard_map/reduce_scatter | solution.py:15
  208.6 1.2 reduce_sum.38
  209.8 1.4 multiply_reduce_fusion
  211.3 0.0 copy-done.1
  211.3 0.0 copy-done.2
  211.3 0.0 copy-done.3
  211.3 2.3 %convolution_multiply_fusion = f32[16,64,128]{2,1,0:T(8,128)} fusion(f32[16,64,128]{2,1,0:T(8,128)S(1)} %bitcast.33, f32[1,16,64,128]{3,2,1,0:T(8,128)} %reduce-scatter.5.cloned.1.call-done, f32[128]{0:T(128)S(1)} %copy-done.2, f32[128]{0:T(128)S(1)} %copy-done.3, f32[16,64]{1,0:T(8,128)S(1)} %add_rsqrt_fusion, f32[16,64]{1,0:T(8,128)S(1)} %broadcast_multiply_fusion, ...), kind=kOutput, calls=%fused_computation.1 | convolution fusion | flops 34340864 | bytes 1614848 | tf_op jit(solution)/shard_map/dot_general | solution.py:66
  (6 shorter events, 0.0 us)
Async XLA Ops:
  6.5 4.9 %copy-start = (bf16[128,512]{1,0:T(8,128)(2,1)S(1)}, bf16[128,512]{1,0:T(8,128)(2,1)}, u32[]{:S(2)}) copy-start(bf16[128,512]{1,0:T(8,128)(2,1)} %param.13) | copy-start | bytes 393220
  6.5 81.3 %all-gather.2.cloned.1.call-start = ((), (), s32[]{:S(2)}) async-start(), calls=%async_computation.2 | async-start | bytes 8650752 | tf_op jit(solution)/shard_map/all_gather | solution.py:61
  12.9 165.0 %reduce-scatter.3.cloned.1.call-start = ((), (), s32[]{:S(2)}) async-start(), calls=%async_computation.3 | async-start | bytes 5242880 | tf_op jit(solution)/shard_map/reduce_scatter | solution.py:15
  130.9 46.9 %copy-start.4 = (bf16[128,128]{1,0:T(8,128)(2,1)S(1)}, bf16[128,128]{1,0:T(8,128)(2,1)}, u32[]{:S(2)}) copy-start(bf16[128,128]{1,0:T(8,128)(2,1)} %param.14) | copy-start | bytes 98308
  130.9 80.3 %copy-start.1 = (bf16[128,128]{1,0:T(8,128)(2,1)S(1)}, bf16[128,128]{1,0:T(8,128)(2,1)}, u32[]{:S(2)}) copy-start(bf16[128,128]{1,0:T(8,128)(2,1)} %param.17) | copy-start | bytes 98308
  130.9 80.3 %copy-start.2 = (f32[128]{0:T(128)S(1)}, f32[128]{0:T(128)}, u32[]{:S(2)}) copy-start(f32[128]{0:T(128)} %param.16) | copy-start | bytes 1540
  130.9 80.3 %copy-start.3 = (f32[128]{0:T(128)S(1)}, f32[128]{0:T(128)}, u32[]{:S(2)}) copy-start(f32[128]{0:T(128)} %param.15) | copy-start | bytes 1540
  131.0 77.6 %reduce-scatter.5.cloned.1.call-start = ((), (), s32[]{:S(2)}) async-start(), calls=%async_computation.4 | async-start | bytes 1572864 | tf_op jit(solution)/shard_map/reduce_scatter | solution.py:15
Sparse Core Ops, SparseCore 0:
  13.0 74.7 all-gather.1
  131.1 46.7 reduce-scatter.2
  180.4 28.1 reduce-scatter.4
where the time goes:
time: 222 us; the launch traced here: 220 us
  waiting for transfers between devices  152 us (68%)
  local copies, waits for them, and re-layouts  34.2 us (15%)
  between operations  13.2 us (6%)
  matrix products  12.4 us (6%)
  other arithmetic  8.54 us (4%)
    reduce_scatter x2, waiting for transfers between devices, own_block(): blocks = lax.psum_scatter(blocks, axes[k], scatter_dimension=0, tiled=True)  77.2 us
    all_gather x1, waiting for transfers between devices, local(): lax.all_gather(right_side, 'row', axis=0, tiled=True)  74.5 us
    all_gather x1, local copies, waits for them, and re-layouts, local(): lax.all_gather(right_side, 'row', axis=0, tiled=True)  23.7 us
    dot_general x1, matrix products, local(): jnp.einsum('ikc,jkc->ijc', left_side, lax.all_gather(right_side, 'row', a...  9.36 us
    transpose x1, local copies, waits for them, and re-layouts, local(): jnp.einsum('ikc,jkc->ijc', left_side, lax.all_gather(right_side, 'row', a...  5.29 us
    transpose x1, local copies, waits for them, and re-layouts, own_block(): jnp.moveaxis(blocks, sequence, range(len(axes))).reshape(-1, *inside)  4.74 us
  transfers between devices with their start and end apart: 3, of which 3 were waited for; matrix products, arithmetic and copies ran while one was open for 0% of the time, Pallas kernels for 0%

commit v1 on v0

v1 whole, which is shorter than its diff:
```python
import jax
import jax.numpy as jnp
from jax import lax
from jax.experimental import pallas as pl
from jax.experimental.pallas import tpu as pltpu
from jax.sharding import PartitionSpec as P

MESH = pl.DeviceIdType.MESH
PLANES = 8
QUAD = 4
PEERS = 32
HELD = 4
PITCH = 136
NT = (((1,), (1,)), ((), ()))
TN = (((0,), (0,)), ((), ()))


def dot(a, b, dims):
    return lax.dot_general(a, b, dims, preferred_element_type=jnp.float32)


def halves(a, b):
    low = lax.broadcasted_iota(jnp.int32, a.shape, 1) < 64
    return jnp.where(low, a, pltpu.roll(b, 64, 1)), jnp.where(low, pltpu.roll(a, 64, 1), b)


def kernel(
    x_ref, mask_ref, in_gain, in_bias, w_proj, w_gate, out_gain, out_bias, w_out, out_ref,
    stage, normed, gate, send_r, send_l, recv_r, recv_l, left, right, s_send, s_recv,
    send_r_sem, recv_r_sem, send_l_sem, recv_l_sem, up_s, up_r, down_s, down_r, s_s, s_r,
):
    row, col = lax.axis_index("row"), lax.axis_index("col")
    z, quarter = lax.div(row, QUAD), lax.rem(row, QUAD)
    me = col * QUAD + quarter
    above = {"row": lax.rem(row + QUAD, PLANES * QUAD), "col": col}
    below = {"row": lax.rem(row + (PLANES - 1) * QUAD, PLANES * QUAD), "col": col}

    def peer(other):
        return {"row": z * QUAD + lax.rem(other, QUAD), "col": lax.div(other, QUAD)}

    def others(step):
        def run(o, carry):
            step(lax.rem(me + o, PEERS))
            return carry

        lax.fori_loop(1, PEERS, run, 0)

    barrier = pltpu.get_barrier_semaphore()
    others(lambda o: pl.semaphore_signal(barrier, inc=1, device_id=peer(o), device_id_type=MESH))
    for neighbour in (above, below):
        pl.semaphore_signal(barrier, inc=1, device_id=neighbour, device_id_type=MESH)

    lane_low = lax.broadcasted_iota(jnp.int32, (8, 128), 1) < 64
    mask = mask_ref[...].astype(jnp.float32)
    masked = jnp.concatenate([mask[:8], mask[8:]], axis=1)
    weights = jnp.transpose(w_proj[...].astype(jnp.float32)).astype(jnp.bfloat16)

    def layer_norm_in(t):
        v = jnp.concatenate([x_ref[t], x_ref[t + 8]], axis=0)
        average = jnp.mean(v, axis=1, keepdims=True)
        variance = jnp.mean(jnp.square(v - average), axis=1, keepdims=True)
        return ((v - average) * lax.rsqrt(variance + 1e-05) * in_gain[...] + in_bias[...]).astype(jnp.bfloat16)

    def project(t, first):
        p = dot(weights[first : first + 256], normed[t], NT)
        side = masked[t : t + 1] * jax.nn.sigmoid(p[:128]) * p[128:]
        stage[pl.ds(t * PITCH, 128), :] = side

    def pack(send):
        for g in range(64):
            pair = [stage[pl.ds(2 * g + e, 8, stride=PITCH), :] for e in range(2)]
            send[g // 2, g % 2] = jnp.concatenate(pair, axis=0).astype(jnp.bfloat16)

    def hand_over(send, recv, send_sem, recv_sem, other):
        return pltpu.make_async_remote_copy(
            src_ref=send.at[other], dst_ref=recv.at[me], send_sem=send_sem.at[other], recv_sem=recv_sem.at[me],
            device_id=peer(other), device_id_type=MESH,
        )

    def arrival(recv, send_sem, recv_sem, other):
        return pltpu.make_async_remote_copy(
            src_ref=recv.at[other], dst_ref=recv.at[other], send_sem=send_sem.at[other], recv_sem=recv_sem.at[other],
            device_id=peer(other), device_id_type=MESH,
        )

    def regroup(recv, store):
        for g in range(2):
            for kp in range(4):
                for rr in range(QUAD):
                    a = recv[8 * kp + rr, g].astype(jnp.float32)
                    b = recv[8 * kp + 4 + rr, g].astype(jnp.float32)
                    first, second = halves(a, b)
                    for e in range(2):
                        rows = slice(8 * e, 8 * e + 8)
                        tile = jnp.concatenate([first[rows], second[rows]], axis=0).astype(jnp.bfloat16)
                        store(2 * g + e, slice(16 * rr, 16 * rr + 16), slice(128 * kp, 128 * kp + 128), tile)

    for t in range(8):
        normed[t] = layer_norm_in(t)
        project(t, 256)
    pack(send_r)
    pl.semaphore_wait(barrier, PEERS - 1 + 2)
    others(lambda o: hand_over(send_r, recv_r, send_r_sem, recv_r_sem, o).start())
    recv_r[me] = send_r[me]

    for t in range(8):
        project(t, 0)
    pack(send_l)
    others(lambda o: hand_over(send_l, recv_l, send_l_sem, recv_l_sem, o).start())
    recv_l[me] = send_l[me]

    others(lambda o: arrival(recv_r, send_r_sem, recv_r_sem, o).wait_recv())

    def store_right(ch, rows, lanes, tile):
        right[z, ch, rows, lanes] = tile

    def up(d, ch):
        block = lax.rem(z + PLANES - d + 1, PLANES)
        return pltpu.make_async_remote_copy(
            src_ref=right.at[block, ch], dst_ref=right.at[block, ch], send_sem=up_s.at[d - 1, ch],
            recv_sem=up_r.at[d - 1, ch], device_id=above, device_id_type=MESH,
        )

    def down(d, ch):
        block = lax.rem(z + d - 1, PLANES)
        return pltpu.make_async_remote_copy(
            src_ref=right.at[block, ch], dst_ref=right.at[block, ch], send_sem=down_s.at[d - 1, ch],
            recv_sem=down_r.at[d - 1, ch], device_id=below, device_id_type=MESH,
        )

    regroup(recv_r, store_right)
    for ch in range(HELD):
        up(1, ch).start()
        down(1, ch).start()

    for t in range(8):
        p = jax.nn.sigmoid(dot(normed[t], w_gate[...], (((1,), (0,)), ((), ()))))
        gate[t] = p[:64]
        gate[t + 8] = p[64:]

    others(lambda o: arrival(recv_l, send_l_sem, recv_l_sem, o).wait_recv())

    def store_left(ch, rows, lanes, tile):
        left[ch, rows, lanes] = tile

    regroup(recv_l, store_left)

    def s_copy(block, rr, first, count):
        return pltpu.make_async_remote_copy(
            src_ref=s_send.at[block, rr, pl.ds(first, count)],
            dst_ref=s_recv.at[pl.ds(pl.multiple_of(me * 32 + first, 8), count)],
            send_sem=s_s.at[block, rr], recv_sem=s_r.at[me],
            device_id={"row": z * QUAD + rr, "col": block}, device_id_type=MESH,
        )

    def s_block(block, ch):
        r = right[block, ch]
        s = dot(left[ch], jnp.concatenate([r, r], axis=0), NT)
        for rr in range(QUAD):
            tile = jnp.where(lane_low, s[16 * rr : 16 * rr + 8], s[16 * rr + 8 : 16 * rr + 16])
            mine = jnp.logical_and(block == col, quarter == rr)

            @pl.when(mine)
            def _():
                s_recv[pl.ds(pl.multiple_of(me * 32 + ch * 8, 8), 8), :] = tile

            @pl.when(jnp.logical_not(mine))
            def _():
                s_send[block, rr, pl.ds(pl.multiple_of(ch * 8, 8), 8), :] = tile
                s_copy(block, rr, pl.multiple_of(ch * 8, 8), 8).start()

    def own(ch, carry):
        s_block(z, ch)
        return carry

    lax.fori_loop(0, HELD, own, 0)

    def ring(n, carry):
        d, ch = lax.div(n, HELD) + 1, lax.rem(n, HELD)
        up(d, ch).wait_recv()

        @pl.when(jnp.logical_or(d < 3, ch < 2))
        def _():
            up(d + 1, ch).start()

        down(d, ch).wait_recv()

        @pl.when(jnp.logical_or(d < 3, ch >= 2))
        def _():
            down(d + 1, ch).start()

        s_block(lax.rem(z + PLANES - d, PLANES), ch)
        s_block(lax.rem(z + d, PLANES), ch)
        return carry

    lax.fori_loop(0, 3 * HELD, ring, 0)
    for ch in range(2):
        up(4, ch).wait_recv()
        s_block(lax.rem(z + 4, PLANES), ch)
        down(4, ch + 2).wait_recv()
        s_block(lax.rem(z + 4, PLANES), ch + 2)

    gain = jnp.transpose(jnp.broadcast_to(out_gain[...], (128, 128)))
    bias = jnp.transpose(jnp.broadcast_to(out_bias[...], (128, 128)))

    def s_arrival(o):
        rows = pl.ds(pl.multiple_of(o * 32, 8), 32)
        pltpu.make_async_remote_copy(
            src_ref=s_recv.at[rows], dst_ref=s_recv.at[rows], send_sem=s_s.at[0, 0], recv_sem=s_r.at[o],
            device_id=peer(o), device_id_type=MESH,
        ).wait_recv()

    others(s_arrival)
    for t in range(8):
        v = s_recv[pl.ds(t, 128, stride=8), :]
        average = jnp.mean(v, axis=0, keepdims=True)
        variance = jnp.mean(jnp.square(v - average), axis=0, keepdims=True)
        n = ((v - average) * lax.rsqrt(variance + 1e-05) * gain + bias).astype(jnp.bfloat16)
        y = dot(n, w_out[...], TN)
        out_ref[t] = gate[t] * y[:64]
        out_ref[t + 8] = gate[t + 8] * y[64:]

    def sent(o):
        hand_over(send_r, recv_r, send_r_sem, recv_r_sem, o).wait_send()
        hand_over(send_l, recv_l, send_l_sem, recv_l_sem, o).wait_send()
        s_copy(lax.div(o, QUAD), lax.rem(o, QUAD), 0, 32).wait_send()

    others(sent)

    def ring_sent(n, carry):
        d, ch = lax.div(n, HELD) + 1, lax.rem(n, HELD)
        up(d, ch).wait_send()
        down(d, ch).wait_send()
        return carry

    lax.fori_loop(0, 3 * HELD, ring_sent, 0)
    for ch in range(2):
        up(4, ch).wait_send()
        down(4, ch + 2).wait_send()


def local(pair_map, pair_mask, in_gain, in_bias, w_proj, w_gate, out_gain, out_bias, w_out):
    f32, bf16 = jnp.float32, jnp.bfloat16
    vmem, dma = pltpu.VMEM, pltpu.SemaphoreType.DMA
    return pl.pallas_call(
        kernel,
        out_shape=jax.ShapeDtypeStruct(pair_map.shape, f32),
        in_specs=[pl.BlockSpec(memory_space=vmem)] * 9,
        out_specs=pl.BlockSpec(memory_space=vmem),
        scratch_shapes=[
            vmem((8 * PITCH, 128), f32),
            vmem((8, 128, 128), bf16),
            vmem((16, 64, 128), f32),
            vmem((PEERS, 2, 16, 128), bf16),
            vmem((PEERS, 2, 16, 128), bf16),
            vmem((PEERS, 2, 16, 128), bf16),
            vmem((PEERS, 2, 16, 128), bf16),
            vmem((HELD, 64, 512), bf16),
            vmem((PLANES, HELD, 64, 512), bf16),
            vmem((PLANES, QUAD, 32, 128), f32),
            vmem((1024, 128), f32),
            dma((PEERS,)), dma((PEERS,)), dma((PEERS,)), dma((PEERS,)),
            dma((4, HELD)), dma((4, HELD)), dma((4, HELD)), dma((4, HELD)),
            dma((PLANES, QUAD)), dma((PEERS,)),
        ],
        compiler_params=pltpu.CompilerParams(collective_id=0, has_side_effects=True),
    )(
        pair_map, pair_mask, in_gain.reshape(1, -1), in_bias.reshape(1, -1), w_proj, w_gate,
        out_gain.reshape(1, -1), out_bias.reshape(1, -1), w_out,
    )


def solution(mesh):
    placed = (P("row", "col", None), P("row", "col"), P(), P(), P(), P(), P(), P(), P())
    return jax.shard_map(local, mesh=mesh, in_specs=placed, out_specs=P("row", "col", None), check_vma=False)
```

time: 222 us -> 52.5 us (0.24)
  the two profiles are of different devices: /device:TPU:17 before, /device:TPU:7 now
where the time goes in v1:
time: 52.5 us; the launch traced here: 52.3 us
  Pallas kernels  50.4 us (96%)
  local copies, waits for them, and re-layouts  1.89 us (4%)
    pallas_call x1, Pallas kernels, local(): pl.pallas_call(kernel, out_shape=jax.ShapeDtypeStruct(pair_map.shape, f32...  50.4 us
    unnamed x1, local copies, waits for them, and re-layouts  1.89 us

profile of v1, /device:TPU:7, one launch (start us, length us, event | category | flops | bytes accessed | tf_op | source)
XLA Modules:
  0.0 52.3 jit_solution(11365170675731832517)
XLA Ops:
  0.0 50.4 %shard_map.91 = f32[16,64,128]{2,1,0:T(8,128)} custom-call(f32[16,64,128]{2,1,0:T(8,128)} %x_ref.1, s32[16,64]{1,0:T(8,128)} %mask_ref.1, f32[1,128]{1,0:T(1,128)} %bitcast.4, f32[1,128]{1,0:T(1,128)} %bitcast.5, bf16[128,512]{1,0:T(8,128)(2,1)} %w_proj.1, bf16[128,128]{1,0:T(8,128)(2,1)} %w_gate.1, f32[1,128]{1,0:T(1,128)} %bitcast.6, f32[1,128]{1,0:T(1,128)} %bitcast.7, ...), custom_call_target="tpu_custom_call" | custom-call | tf_op jit(solution)/shard_map/pallas_call | solution.py:245
  50.5 1.9 %copy.11 = f32[16,64,128]{2,1,0:T(8,128)} copy(f32[16,64,128]{2,1,0:T(8,128)} %shard_map.91) | data formatting | bytes 1048576

commit v2 on v1

v2 whole, which is shorter than its diff:
```python
import jax
import jax.numpy as jnp
from jax import lax
from jax.experimental import pallas as pl
from jax.experimental.pallas import tpu as pltpu
from jax.sharding import PartitionSpec as P

MESH = pl.DeviceIdType.MESH
PLANES = 8
QUAD = 4
PEERS = 32
HELD = 4
PITCH = 136
NN = (((1,), (0,)), ((), ()))
NT = (((1,), (1,)), ((), ()))
TN = (((0,), (0,)), ((), ()))


def steps(reach):
    every = [(dx, dy, dh) for dx in range(4) for dy in range(4) for dh in range(2) if dx or dy or dh]
    return sorted(every, key=lambda s: reach(min(s[0], 4 - s[0]) + min(s[1], 4 - s[1])))


def dot(a, b, dims):
    return lax.dot_general(a, b, dims, preferred_element_type=jnp.float32)


def halves(a, b):
    low = lax.broadcasted_iota(jnp.int32, a.shape, 1) < 64
    return jnp.where(low, a, pltpu.roll(b, 64, 1)), jnp.where(low, pltpu.roll(a, 64, 1), b)


def kernel(
    x_hbm, mask_hbm, in_gain_hbm, in_bias_hbm, w_proj_hbm, w_gate_hbm, out_gain_hbm, out_bias_hbm, w_out_hbm, out_ref,
    x_ref, mask_ref, in_gain, in_bias, w_proj, w_gate, out_gain, out_bias, w_out, x_sem, in_sem,
    stage, normed, gate, send_r, send_l, recv_r, recv_l, left, right, s_send, s_recv, column,
    send_r_sem, recv_r_sem, send_l_sem, recv_l_sem, up_s, up_r, down_s, down_r, s_s, s_r,
):
    row, col = lax.axis_index("row"), lax.axis_index("col")
    z, quarter = lax.div(row, QUAD), lax.rem(row, QUAD)
    me = col * QUAD + quarter
    x = lax.div(col, 4) * 2 + lax.div(quarter, 2)
    y, core = lax.rem(col, 4), lax.rem(quarter, 2)
    strip = lax.div(col, 2)
    above = {"row": lax.rem(row + QUAD, PLANES * QUAD), "col": col}
    below = {"row": lax.rem(row + (PLANES - 1) * QUAD, PLANES * QUAD), "col": col}

    def peer(other):
        return {"row": z * QUAD + lax.rem(other, QUAD), "col": lax.div(other, QUAD)}

    def each(reach, step):
        for dx, dy, dh in steps(reach):
            to_x, to_y, to_core = lax.rem(x + dx, 4), lax.rem(y + dy, 4), lax.rem(core + dh, 2)
            step(lax.div(to_x, 2) * 16 + to_y * 4 + lax.rem(to_x, 2) * 2 + to_core)

    barrier = pltpu.get_barrier_semaphore()
    each(lambda hops: -hops, lambda o: pl.semaphore_signal(barrier, inc=1, device_id=peer(o), device_id_type=MESH))
    for neighbour in (above, below):
        pl.semaphore_signal(barrier, inc=1, device_id=neighbour, device_id_type=MESH)

    x_in = [
        pltpu.make_async_copy(x_hbm.at[:, pl.ds(2 * n, 2)], x_ref.at[:, pl.ds(2 * n, 2)], x_sem.at[n]) for n in range(4)
    ]
    small = [
        pltpu.make_async_copy(src, dst, in_sem.at[n])
        for n, (src, dst) in enumerate((
            (in_gain_hbm, in_gain), (in_bias_hbm, in_bias), (w_proj_hbm, w_proj), (mask_hbm, mask_ref),
            (w_gate_hbm, w_gate), (out_gain_hbm, out_gain), (out_bias_hbm, out_bias), (w_out_hbm, w_out),
        ))
    ]
    for copy in small[:4] + x_in + small[4:]:
        copy.start()
    for copy in small[:4]:
        copy.wait()

    lane_low = lax.broadcasted_iota(jnp.int32, (8, 128), 1) < 64
    mask = mask_ref[...].astype(jnp.float32)
    masked = jnp.concatenate([mask[:8], mask[8:]], axis=1)
    weights = jnp.transpose(w_proj[...].astype(jnp.float32)).astype(jnp.bfloat16)

    def layer_norm_in(t):
        v = jnp.concatenate([x_ref[0, t], x_ref[1, t]], axis=0)
        average = jnp.mean(v, axis=1, keepdims=True)
        variance = jnp.mean(jnp.square(v - average), axis=1, keepdims=True)
        return ((v - average) * lax.rsqrt(variance + 1e-05) * in_gain[...] + in_bias[...]).astype(jnp.bfloat16)

    def project(t, first):
        p = dot(weights[first : first + 256], normed[t], NT)
        side = masked[t : t + 1] * jax.nn.sigmoid(p[:128]) * p[128:]
        stage[pl.ds(t * PITCH, 128), :] = side

    def pack(send):
        for g in range(64):
            pair = [stage[pl.ds(2 * g + e, 8, stride=PITCH), :] for e in range(2)]
            send[g // 2, g % 2] = jnp.concatenate(pair, axis=0).astype(jnp.bfloat16)

    def move(src, dst, send_sem, recv_sem, to):
        return pltpu.make_async_remote_copy(
            src_ref=src, dst_ref=dst, send_sem=send_sem, recv_sem=recv_sem, device_id=to, device_id_type=MESH
        )

    def regroup(recv, strip, store):
        for g in range(2):
            for rr in range(QUAD):
                a = recv[8 * strip + rr, g].astype(jnp.float32)
                b = recv[8 * strip + 4 + rr, g].astype(jnp.float32)
                first, second = halves(a, b)
                for e in range(2):
                    rows = slice(8 * e, 8 * e + 8)
                    tile = jnp.concatenate([first[rows], second[rows]], axis=0).astype(jnp.bfloat16)
                    store(2 * g + e, slice(16 * rr, 16 * rr + 16), tile)

    for t in range(8):
        if t % 2 == 0:
            x_in[t // 2].wait()
        normed[t] = layer_norm_in(t)
        project(t, 256)
    pack(send_r)
    pl.semaphore_wait(barrier, PEERS - 1 + 2)
    each(
        lambda hops: (1, 2, 3, 4, 0)[hops],
        lambda o: move(send_r.at[o], recv_r.at[me], send_r_sem, recv_r_sem.at[strip], peer(o)).start(),
    )
    recv_r[me] = send_r[me]

    for t in range(8):
        project(t, 0)
    pack(send_l)
    each(
        lambda hops: -hops,
        lambda o: move(send_l.at[o], recv_l.at[me], send_l_sem, recv_l_sem, peer(o)).start(),
    )
    recv_l[me] = send_l[me]

    for copy in small[4:]:
        copy.wait()
    for t in range(8):
        p = jax.nn.sigmoid(dot(normed[t], w_gate[...], NN))
        gate[t] = p[:64]
        gate[t + 8] = p[64:]
    column[0] = jnp.transpose(jnp.broadcast_to(out_gain[...], (128, 128)))
    column[1] = jnp.transpose(jnp.broadcast_to(out_bias[...], (128, 128)))

    def near(e):
        return lax.rem(lax.div(strip, 2) + e // 2, 2) * 2 + lax.rem(strip + e % 2, 2)

    def up(d, e):
        piece = right.at[lax.rem(z + PLANES - d + 1, PLANES) * 4 + near(e)]
        return move(piece, piece, up_s, up_r.at[d - 1, e], above)

    def down(d, e):
        piece = right.at[lax.rem(z + d - 1, PLANES) * 4 + near(e)]
        return move(piece, piece, down_s, down_r.at[d - 1, e], below)

    for e in range(4):
        got = near(e)
        arrived = recv_r.at[pl.ds(8 * got, 8 if e else 7)]
        move(arrived, arrived, send_r_sem, recv_r_sem.at[got], above).wait_recv()

        def store_right(ch, rows, tile, got=got):
            right[z * 4 + got, ch, rows] = tile

        regroup(recv_r, got, store_right)
        up(1, e).start()
        down(1, e).start()

    def store_left(strip):
        def store(ch, rows, tile):
            left[ch, rows, slice(128 * strip, 128 * strip + 128)] = tile

        return store

    def s_block(block, ch):
        r = jnp.concatenate([right[block * 4 + k, ch] for k in range(4)], axis=1)
        s = dot(left[ch], jnp.concatenate([r, r], axis=0), NT)
        for rr in range(QUAD):
            tile = jnp.where(lane_low, s[16 * rr : 16 * rr + 8], s[16 * rr + 8 : 16 * rr + 16])
            mine = jnp.logical_and(block == col, quarter == rr)
            dst = s_recv.at[pl.ds(pl.multiple_of(me * 32 + ch * 8, 8), 8)]

            @pl.when(mine)
            def _():
                dst[...] = tile

            @pl.when(jnp.logical_not(mine))
            def _():
                src = s_send.at[pl.ds(pl.multiple_of((block * QUAD + rr) * 32 + ch * 8, 8), 8)]
                src[...] = tile
                move(src, dst, s_s, s_r, {"row": z * QUAD + rr, "col": block}).start()

    def pair(d, ch):
        s_block(lax.rem(z + PLANES - d, PLANES), ch)
        s_block(lax.rem(z + d, PLANES), ch)

    def forward(d, e):
        up(d, e).wait_recv()
        if d < 3 or e < 2:
            up(d + 1, e).start()
        down(d, e).wait_recv()
        if d < 3 or e >= 2:
            down(d + 1, e).start()

    forward(1, 0)
    forward(1, 1)
    arrived = recv_l.at[pl.ds(0, PEERS - 1)]
    move(arrived, arrived, send_l_sem, recv_l_sem, above).wait_recv()
    for k in range(4):
        regroup(recv_l, k, store_left(k))
    for e in range(2, 4):
        forward(1, e)
        for ch in range(2 * e - 4, 2 * e - 2):
            s_block(z, ch)
    for d in range(2, 4):
        for e in range(4):
            forward(d, e)
            pair(d - 1, e)
    for n in range(2):
        pair(3, 2 * n)
        pair(3, 2 * n + 1)
        up(4, n).wait_recv()
        down(4, n + 2).wait_recv()
    for ch in range(HELD):
        s_block(lax.rem(z + 4, PLANES), ch)

    sent = send_r.at[pl.ds(0, PEERS - 1)]
    move(sent, sent, send_r_sem, recv_r_sem.at[0], above).wait_send()
    move(sent, sent, send_l_sem, recv_l_sem, above).wait_send()
    sent = right.at[pl.ds(0, 14)]
    move(sent, sent, up_s, up_r.at[0, 0], above).wait_send()
    move(sent, sent, down_s, down_r.at[0, 0], below).wait_send()
    sent = s_send.at[pl.ds(0, (PEERS - 1) * 32)]
    move(sent, sent, s_s, s_r, above).wait_send()
    arrived = s_recv.at[pl.ds(0, (PEERS - 1) * 32)]
    move(arrived, arrived, s_s, s_r, above).wait_recv()
    for t in range(8):
        v = s_recv[pl.ds(t, 128, stride=8), :]
        average = jnp.mean(v, axis=0, keepdims=True)
        variance = jnp.mean(jnp.square(v - average), axis=0, keepdims=True)
        n = ((v - average) * lax.rsqrt(variance + 1e-05) * column[0] + column[1]).astype(jnp.bfloat16)
        o = dot(n, w_out[...], TN)
        out_ref[0, t] = gate[t] * o[:64]
        out_ref[1, t] = gate[t + 8] * o[64:]


def local(pair_map, pair_mask, in_gain, in_bias, w_proj, w_gate, out_gain, out_bias, w_out):
    f32, bf16 = jnp.float32, jnp.bfloat16
    vmem, dma = pltpu.VMEM, pltpu.SemaphoreType.DMA
    split = (2, 8, 64, 128)
    args = (
        pair_map.reshape(split), pair_mask, in_gain.reshape(1, -1), in_bias.reshape(1, -1), w_proj, w_gate,
        out_gain.reshape(1, -1), out_bias.reshape(1, -1), w_out,
    )
    out = pl.pallas_call(
        kernel,
        out_shape=jax.ShapeDtypeStruct(split, f32),
        in_specs=[pl.BlockSpec(memory_space=pltpu.HBM)] * 9,
        out_specs=pl.BlockSpec(memory_space=vmem),
        scratch_shapes=[
            *(vmem(a.shape, a.dtype) for a in args),
            dma((4,)), dma((8,)),
            vmem((8 * PITCH, 128), f32),
            vmem((8, 128, 128), bf16),
            vmem((16, 64, 128), f32),
            vmem((PEERS, 2, 16, 128), bf16),
            vmem((PEERS, 2, 16, 128), bf16),
            vmem((PEERS, 2, 16, 128), bf16),
            vmem((PEERS, 2, 16, 128), bf16),
            vmem((HELD, 64, 512), bf16),
            vmem((PLANES * 4, HELD, 64, 128), bf16),
            vmem((1024, 128), f32),
            vmem((1024, 128), f32),
            vmem((2, 128, 128), f32),
            dma, dma((4,)), dma, dma, dma, dma((4, 4)), dma, dma((4, 4)), dma, dma,
        ],
        compiler_params=pltpu.CompilerParams(
            collective_id=0, has_side_effects=True, vmem_limit_bytes=24 * 1024 * 1024
        ),
    )(*(pltpu.with_memory_space_constraint(a, pltpu.HBM) for a in args))
    return out.reshape(pair_map.shape)


def solution(mesh):
    placed = (P("row", "col", None), P("row", "col"), P(), P(), P(), P(), P(), P(), P())
    return jax.shard_map(local, mesh=mesh, in_specs=placed, out_specs=P("row", "col", None), check_vma=False)
```

time: 52.5 us -> 45.9 us (0.87)
  the two profiles are of different devices: /device:TPU:7 before, /device:TPU:5 now
where the time goes in v2:
time: 45.9 us; the launch traced here: 45.8 us
  Pallas kernels  45 us (98%)
  local copies, waits for them, and re-layouts  0.8 us (2%)
    pallas_call x1, Pallas kernels, local(): pl.pallas_call(kernel, out_shape=jax.ShapeDtypeStruct(split, f32), in_spe...  45 us

profile of v2, /device:TPU:5, one launch (start us, length us, event | category | flops | bytes accessed | tf_op | source)
XLA Modules:
  0.0 45.8 jit_solution(3350609516249617923)
XLA Ops:
  0.0 45.0 %shard_map.91 = f32[2,8,64,128]{3,2,1,0:T(8,128)S(1)} custom-call(f32[2,8,64,128]{3,2,1,0:T(8,128)} %bitcast.7, s32[16,64]{1,0:T(8,128)} %mask_hbm.1, f32[1,128]{1,0:T(1,128)} %bitcast.8, f32[1,128]{1,0:T(1,128)} %bitcast.9, bf16[128,512]{1,0:T(8,128)(2,1)} %w_proj_hbm.1, bf16[128,128]{1,0:T(8,128)(2,1)} %w_gate_hbm.1, f32[1,128]{1,0:T(1,128)} %bitcast.10, ...), custom_call_target="tpu_custom_call" | custom-call | tf_op jit(solution)/shard_map/pallas_call | solution.py:253
  45.0 0.8 %copy.11 = f32[16,64,128]{2,1,0:T(8,128)} copy(f32[16,64,128]{2,1,0:T(8,128)S(1)} %bitcast.6) | data formatting | bytes 1048576

commit v3 on v2

--- a/solution.py
+++ b/solution.py
@@ -53,14 +53,7 @@
             to_x, to_y, to_core = lax.rem(x + dx, 4), lax.rem(y + dy, 4), lax.rem(core + dh, 2)
             step(lax.div(to_x, 2) * 16 + to_y * 4 + lax.rem(to_x, 2) * 2 + to_core)
 
-    barrier = pltpu.get_barrier_semaphore()
-    each(lambda hops: -hops, lambda o: pl.semaphore_signal(barrier, inc=1, device_id=peer(o), device_id_type=MESH))
-    for neighbour in (above, below):
-        pl.semaphore_signal(barrier, inc=1, device_id=neighbour, device_id_type=MESH)
-
-    x_in = [
-        pltpu.make_async_copy(x_hbm.at[:, pl.ds(2 * n, 2)], x_ref.at[:, pl.ds(2 * n, 2)], x_sem.at[n]) for n in range(4)
-    ]
+    x_in = pltpu.make_async_copy(x_hbm, x_ref, x_sem)
     small = [
         pltpu.make_async_copy(src, dst, in_sem.at[n])
         for n, (src, dst) in enumerate((
@@ -68,8 +61,13 @@
             (w_gate_hbm, w_gate), (out_gain_hbm, out_gain), (out_bias_hbm, out_bias), (w_out_hbm, w_out),
         ))
     ]
-    for copy in small[:4] + x_in + small[4:]:
+    for copy in (*small[:4], x_in, *small[4:]):
         copy.start()
+    barrier = pltpu.get_barrier_semaphore()
+    each(lambda hops: -hops, lambda o: pl.semaphore_signal(barrier, inc=1, device_id=peer(o), device_id_type=MESH))
+    for neighbour in (above, below):
+        pl.semaphore_signal(barrier, inc=1, device_id=neighbour, device_id_type=MESH)
+
     for copy in small[:4]:
         copy.wait()
 
@@ -110,9 +108,8 @@
                     tile = jnp.concatenate([first[rows], second[rows]], axis=0).astype(jnp.bfloat16)
                     store(2 * g + e, slice(16 * rr, 16 * rr + 16), tile)
 
+    x_in.wait()
     for t in range(8):
-        if t % 2 == 0:
-            x_in[t // 2].wait()
         normed[t] = layer_norm_in(t)
         project(t, 256)
     pack(send_r)
@@ -126,10 +123,6 @@
     for t in range(8):
         project(t, 0)
     pack(send_l)
-    each(
-        lambda hops: -hops,
-        lambda o: move(send_l.at[o], recv_l.at[me], send_l_sem, recv_l_sem, peer(o)).start(),
-    )
     recv_l[me] = send_l[me]
 
     for copy in small[4:]:
@@ -144,13 +137,25 @@
     def near(e):
         return lax.rem(lax.div(strip, 2) + e // 2, 2) * 2 + lax.rem(strip + e % 2, 2)
 
-    def up(d, e):
-        piece = right.at[lax.rem(z + PLANES - d + 1, PLANES) * 4 + near(e)]
-        return move(piece, piece, up_s, up_r.at[d - 1, e], above)
-
-    def down(d, e):
-        piece = right.at[lax.rem(z + d - 1, PLANES) * 4 + near(e)]
-        return move(piece, piece, down_s, down_r.at[d - 1, e], below)
+    class Stream:
+        def __init__(self, sign, to, far, sends, recvs):
+            self.sign, self.to, self.far, self.sends, self.recvs = sign, to, far, sends, recvs
+            self.rest = (2, 3) if far == 0 else (0, 1)
+
+        def block(self, d):
+            return lax.rem(z + (PLANES - d if self.sign > 0 else d), PLANES)
+
+        def copy(self, part, slot):
+            return move(part, part, self.sends, self.recvs.at[slot], self.to)
+
+        def strip(self, d, e):
+            part = right.at[self.block(d - 1) * 4 + near(e)]
+            return self.copy(part if d == 1 else part.at[pl.ds(self.far, 2)], 4 * (d - 1) + e)
+
+        def half(self, n, h):
+            return self.copy(right.at[pl.ds(self.block(1) * 4 + 2 * h, 2), self.rest[n]], 20 + 2 * n + h)
+
+    streams = (Stream(1, above, 0, up_s, up_r), Stream(-1, below, 2, down_s, down_r))
 
     for e in range(4):
         got = near(e)
@@ -161,8 +166,13 @@
             right[z * 4 + got, ch, rows] = tile
 
         regroup(recv_r, got, store_right)
-        up(1, e).start()
-        down(1, e).start()
+        for stream in streams:
+            stream.strip(1, e).start()
+        if e == 0:
+            each(
+                lambda hops: -hops,
+                lambda o: move(send_l.at[o], recv_l.at[me], send_l_sem, recv_l_sem, peer(o)).start(),
+            )
 
     def store_left(strip):
         def store(ch, rows, tile):
@@ -170,13 +180,19 @@
 
         return store
 
-    def s_block(block, ch):
-        r = jnp.concatenate([right[block * 4 + k, ch] for k in range(4)], axis=1)
-        s = dot(left[ch], jnp.concatenate([r, r], axis=0), NT)
+    def s_block(block, channels=range(HELD)):
+        tiles = []
+        for ch in channels:
+            r = jnp.concatenate([right[block * 4 + k, ch] for k in range(4)], axis=1)
+            s = dot(left[ch], jnp.concatenate([r, r], axis=0), NT)
+            tiles.append([
+                jnp.where(lane_low, s[16 * rr : 16 * rr + 8], s[16 * rr + 8 : 16 * rr + 16]) for rr in range(QUAD)
+            ])
+        first, count = channels[0] * 8, len(channels) * 8
+        dst = s_recv.at[pl.ds(pl.multiple_of(me * 32 + first, 8), count)]
         for rr in range(QUAD):
-            tile = jnp.where(lane_low, s[16 * rr : 16 * rr + 8], s[16 * rr + 8 : 16 * rr + 16])
+            tile = jnp.concatenate([t[rr] for t in tiles], axis=0)
             mine = jnp.logical_and(block == col, quarter == rr)
-            dst = s_recv.at[pl.ds(pl.multiple_of(me * 32 + ch * 8, 8), 8)]
 
             @pl.when(mine)
             def _():
@@ -184,50 +200,60 @@
 
             @pl.when(jnp.logical_not(mine))
             def _():
-                src = s_send.at[pl.ds(pl.multiple_of((block * QUAD + rr) * 32 + ch * 8, 8), 8)]
+                src = s_send.at[pl.ds(pl.multiple_of((block * QUAD + rr) * 32 + first, 8), count)]
                 src[...] = tile
                 move(src, dst, s_s, s_r, {"row": z * QUAD + rr, "col": block}).start()
 
-    def pair(d, ch):
-        s_block(lax.rem(z + PLANES - d, PLANES), ch)
-        s_block(lax.rem(z + d, PLANES), ch)
-
-    def forward(d, e):
-        up(d, e).wait_recv()
-        if d < 3 or e < 2:
-            up(d + 1, e).start()
-        down(d, e).wait_recv()
-        if d < 3 or e >= 2:
-            down(d + 1, e).start()
-
-    forward(1, 0)
-    forward(1, 1)
+    def forward(d):
+        for e in range(4):
+            for stream in streams:
+                stream.strip(d, e).wait_recv()
+                if d < 5:
+                    stream.strip(d + 1, e).start()
+
+    def late(n, h):
+        for stream in streams:
+            stream.half(n, h).start()
+
+    def s_late(n):
+        for stream in streams:
+            stream.half(n, 0).wait_recv()
+            stream.half(n, 1).wait_recv()
+            s_block(stream.block(2), (stream.rest[n],))
+
+    def s_far(d):
+        for stream in streams:
+            s_block(stream.block(d), range(stream.far, stream.far + 2))
+
+    forward(1)
+    late(0, 0)
     arrived = recv_l.at[pl.ds(0, PEERS - 1)]
     move(arrived, arrived, send_l_sem, recv_l_sem, above).wait_recv()
     for k in range(4):
         regroup(recv_l, k, store_left(k))
-    for e in range(2, 4):
-        forward(1, e)
-        for ch in range(2 * e - 4, 2 * e - 2):
-            s_block(z, ch)
-    for d in range(2, 4):
-        for e in range(4):
-            forward(d, e)
-            pair(d - 1, e)
-    for n in range(2):
-        pair(3, 2 * n)
-        pair(3, 2 * n + 1)
-        up(4, n).wait_recv()
-        down(4, n + 2).wait_recv()
-    for ch in range(HELD):
-        s_block(lax.rem(z + 4, PLANES), ch)
+    s_block(z)
+    forward(2)
+    late(0, 1)
+    for stream in streams:
+        s_block(stream.block(1))
+    forward(3)
+    late(1, 0)
+    s_far(2)
+    s_far(3)
+    forward(4)
+    late(1, 1)
+    s_late(0)
+    s_far(4)
+    forward(5)
+    s_far(5)
+    s_late(1)
 
     sent = send_r.at[pl.ds(0, PEERS - 1)]
     move(sent, sent, send_r_sem, recv_r_sem.at[0], above).wait_send()
     move(sent, sent, send_l_sem, recv_l_sem, above).wait_send()
     sent = right.at[pl.ds(0, 14)]
-    move(sent, sent, up_s, up_r.at[0, 0], above).wait_send()
-    move(sent, sent, down_s, down_r.at[0, 0], below).wait_send()
+    move(sent, sent, up_s, up_r.at[0], above).wait_send()
+    move(sent, sent, down_s, down_r.at[0], below).wait_send()
     sent = s_send.at[pl.ds(0, (PEERS - 1) * 32)]
     move(sent, sent, s_s, s_r, above).wait_send()
     arrived = s_recv.at[pl.ds(0, (PEERS - 1) * 32)]
@@ -257,7 +283,7 @@
         out_specs=pl.BlockSpec(memory_space=vmem),
         scratch_shapes=[
             *(vmem(a.shape, a.dtype) for a in args),
-            dma((4,)), dma((8,)),
+            dma, dma((8,)),
             vmem((8 * PITCH, 128), f32),
             vmem((8, 128, 128), bf16),
             vmem((16, 64, 128), f32),
@@ -270,7 +296,7 @@
             vmem((1024, 128), f32),
             vmem((1024, 128), f32),
             vmem((2, 128, 128), f32),
-            dma, dma((4,)), dma, dma, dma, dma((4, 4)), dma, dma((4, 4)), dma, dma,
+            dma, dma((4,)), dma, dma, dma, dma((24,)), dma, dma((24,)), dma, dma,
         ],
         compiler_params=pltpu.CompilerParams(
             collective_id=0, has_side_effects=True, vmem_limit_bytes=24 * 1024 * 1024

time: 45.9 us -> 42.7 us (0.930)
  the two profiles are of different devices: /device:TPU:5 before, /device:TPU:17 now
where the time goes in v3:
time: 42.7 us; the launch traced here: 42.6 us
  Pallas kernels  41.8 us (98%)
  local copies, waits for them, and re-layouts  0.8 us (2%)
    pallas_call x1, Pallas kernels, local(): pl.pallas_call(kernel, out_shape=jax.ShapeDtypeStruct(split, f32), in_spe...  41.8 us

profile of v3, /device:TPU:17, one launch (start us, length us, event | category | flops | bytes accessed | tf_op | source)
XLA Modules:
  0.0 42.6 jit_solution(205733724955109406)
XLA Ops:
  0.0 41.8 %shard_map.91 = f32[2,8,64,128]{3,2,1,0:T(8,128)S(1)} custom-call(f32[2,8,64,128]{3,2,1,0:T(8,128)} %bitcast.7, s32[16,64]{1,0:T(8,128)} %mask_hbm.1, f32[1,128]{1,0:T(1,128)} %bitcast.8, f32[1,128]{1,0:T(1,128)} %bitcast.9, bf16[128,512]{1,0:T(8,128)(2,1)} %w_proj_hbm.1, bf16[128,128]{1,0:T(8,128)(2,1)} %w_gate_hbm.1, f32[1,128]{1,0:T(1,128)} %bitcast.10, ...), custom_call_target="tpu_custom_call" | custom-call | tf_op jit(solution)/shard_map/pallas_call | solution.py:279
  41.8 0.8 %copy.11 = f32[16,64,128]{2,1,0:T(8,128)} copy(f32[16,64,128]{2,1,0:T(8,128)S(1)} %bitcast.6) | data formatting | bytes 1048576

commit v4 on v3

--- a/solution.py
+++ b/solution.py
@@ -33,8 +33,8 @@
 def kernel(
     x_hbm, mask_hbm, in_gain_hbm, in_bias_hbm, w_proj_hbm, w_gate_hbm, out_gain_hbm, out_bias_hbm, w_out_hbm, out_ref,
     x_ref, mask_ref, in_gain, in_bias, w_proj, w_gate, out_gain, out_bias, w_out, x_sem, in_sem,
-    stage, normed, gate, send_r, send_l, recv_r, recv_l, left, right, s_send, s_recv, column,
-    send_r_sem, recv_r_sem, send_l_sem, recv_l_sem, up_s, up_r, down_s, down_r, s_s, s_r,
+    stage, normed, gate, send_r, send_l, recv_r, recv_l, raw, recv_x, left, right, s_send, s_recv, column,
+    send_r_sem, recv_r_sem, send_l_sem, recv_l_sem, send_x_sem, recv_x_sem, up_s, up_r, down_s, down_r, s_s, s_r,
 ):
     row, col = lax.axis_index("row"), lax.axis_index("col")
     z, quarter = lax.div(row, QUAD), lax.rem(row, QUAD)
@@ -108,12 +108,48 @@
                     tile = jnp.concatenate([first[rows], second[rows]], axis=0).astype(jnp.bfloat16)
                     store(2 * g + e, slice(16 * rr, 16 * rr + 16), tile)
 
+    def near(e):
+        return lax.rem(lax.div(strip, 2) + e // 2, 2) * 2 + lax.rem(strip + e % 2, 2)
+
+    class Stream:
+        def __init__(self, sign, to, far, sends, recvs):
+            self.sign, self.to, self.far, self.sends, self.recvs = sign, to, far, sends, recvs
+            self.rest = (2, 3) if far == 0 else (0, 1)
+
+        def block(self, d):
+            return lax.rem(z + (PLANES - d if self.sign > 0 else d), PLANES)
+
+        def raw(self, e):
+            at = pl.ds(8 * near(e), 8)
+            src, dst = send_r.at[at, self.rest[0] // 2], raw.at[at, self.far // 2]
+            return move(src, dst, self.sends, self.recvs.at[24 + e], self.to)
+
+        def strip(self, d, e):
+            part = right.at[self.block(d - 1) * 4 + near(e), pl.ds(self.far, 2)]
+            return move(part, part, self.sends, self.recvs.at[4 * (d - 1) + e], self.to)
+
+        def half(self, n, h):
+            part = right.at[pl.ds(self.block(1) * 4 + 2 * h, 2), self.rest[n]]
+            return move(part, part, self.sends, self.recvs.at[20 + 2 * n + h], self.to)
+
+    streams = (Stream(1, above, 0, up_s, up_r), Stream(-1, below, 2, down_s, down_r))
+
+    def pass_on(e):
+        for stream in streams:
+            stream.raw(e).wait_recv()
+        for n in range(0 if e else 1, 8):
+            o = 8 * near(e) + lax.rem(me + n, 8)
+            move(raw.at[o], recv_x.at[me], send_x_sem, recv_x_sem, peer(o)).start()
+
     x_in.wait()
     for t in range(8):
         normed[t] = layer_norm_in(t)
         project(t, 256)
     pack(send_r)
     pl.semaphore_wait(barrier, PEERS - 1 + 2)
+    for e in (3, 2, 1, 0):
+        for stream in streams:
+            stream.raw(e).start()
     each(
         lambda hops: (1, 2, 3, 4, 0)[hops],
         lambda o: move(send_r.at[o], recv_r.at[me], send_r_sem, recv_r_sem.at[strip], peer(o)).start(),
@@ -134,29 +170,6 @@
     column[0] = jnp.transpose(jnp.broadcast_to(out_gain[...], (128, 128)))
     column[1] = jnp.transpose(jnp.broadcast_to(out_bias[...], (128, 128)))
 
-    def near(e):
-        return lax.rem(lax.div(strip, 2) + e // 2, 2) * 2 + lax.rem(strip + e % 2, 2)
-
-    class Stream:
-        def __init__(self, sign, to, far, sends, recvs):
-            self.sign, self.to, self.far, self.sends, self.recvs = sign, to, far, sends, recvs
-            self.rest = (2, 3) if far == 0 else (0, 1)
-
-        def block(self, d):
-            return lax.rem(z + (PLANES - d if self.sign > 0 else d), PLANES)
-
-        def copy(self, part, slot):
-            return move(part, part, self.sends, self.recvs.at[slot], self.to)
-
-        def strip(self, d, e):
-            part = right.at[self.block(d - 1) * 4 + near(e)]
-            return self.copy(part if d == 1 else part.at[pl.ds(self.far, 2)], 4 * (d - 1) + e)
-
-        def half(self, n, h):
-            return self.copy(right.at[pl.ds(self.block(1) * 4 + 2 * h, 2), self.rest[n]], 20 + 2 * n + h)
-
-    streams = (Stream(1, above, 0, up_s, up_r), Stream(-1, below, 2, down_s, down_r))
-
     for e in range(4):
         got = near(e)
         arrived = recv_r.at[pl.ds(8 * got, 8 if e else 7)]
@@ -169,6 +182,12 @@
         for stream in streams:
             stream.strip(1, e).start()
         if e == 0:
+            pass_on(3)
+            pass_on(2)
+        if e == 2:
+            pass_on(1)
+            pass_on(0)
+            recv_x[me] = raw[me]
             each(
                 lambda hops: -hops,
                 lambda o: move(send_l.at[o], recv_l.at[me], send_l_sem, recv_l_sem, peer(o)).start(),
@@ -226,22 +245,31 @@
             s_block(stream.block(d), range(stream.far, stream.far + 2))
 
     forward(1)
+    forward(2)
+    arrived = recv_x.at[pl.ds(0, PEERS - 1)]
+    move(arrived, arrived, send_x_sem, recv_x_sem, above).wait_recv()
+    for k in range(4):
+
+        def store_next(ch, rows, tile, k=k):
+            stream = streams[ch // 2]
+            right[stream.block(1) * 4 + k, stream.rest[ch % 2], rows] = tile
+
+        regroup(recv_x, k, store_next)
     late(0, 0)
+    late(0, 1)
     arrived = recv_l.at[pl.ds(0, PEERS - 1)]
     move(arrived, arrived, send_l_sem, recv_l_sem, above).wait_recv()
     for k in range(4):
         regroup(recv_l, k, store_left(k))
     s_block(z)
-    forward(2)
-    late(0, 1)
+    forward(3)
+    late(1, 0)
     for stream in streams:
         s_block(stream.block(1))
-    forward(3)
-    late(1, 0)
     s_far(2)
-    s_far(3)
     forward(4)
     late(1, 1)
+    s_far(3)
     s_late(0)
     s_far(4)
     forward(5)
@@ -251,6 +279,7 @@
     sent = send_r.at[pl.ds(0, PEERS - 1)]
     move(sent, sent, send_r_sem, recv_r_sem.at[0], above).wait_send()
     move(sent, sent, send_l_sem, recv_l_sem, above).wait_send()
+    move(sent, sent, send_x_sem, recv_x_sem, above).wait_send()
     sent = right.at[pl.ds(0, 14)]
     move(sent, sent, up_s, up_r.at[0], above).wait_send()
     move(sent, sent, down_s, down_r.at[0], below).wait_send()
@@ -291,12 +320,14 @@
             vmem((PEERS, 2, 16, 128), bf16),
             vmem((PEERS, 2, 16, 128), bf16),
             vmem((PEERS, 2, 16, 128), bf16),
+            vmem((PEERS, 2, 16, 128), bf16),
+            vmem((PEERS, 2, 16, 128), bf16),
             vmem((HELD, 64, 512), bf16),
             vmem((PLANES * 4, HELD, 64, 128), bf16),
             vmem((1024, 128), f32),
             vmem((1024, 128), f32),
             vmem((2, 128, 128), f32),
-            dma, dma((4,)), dma, dma, dma, dma((24,)), dma, dma((24,)), dma, dma,
+            dma, dma((4,)), dma, dma, dma, dma, dma, dma((28,)), dma, dma((28,)), dma, dma,
         ],
         compiler_params=pltpu.CompilerParams(
             collective_id=0, has_side_effects=True, vmem_limit_bytes=24 * 1024 * 1024

time: 42.7 us -> 41 us (0.960)
  Pallas kernels: 41.8 us -> 40.1 us
    pallas_call x1, Pallas kernels: 41.8 us -> 40.1 us  [local(): pl.pallas_call(kernel, out_shape=jax.ShapeDtypeStruct(split, f32), in_spe...]
where the time goes in v4:
time: 41 us; the launch traced here: 40.9 us
  Pallas kernels  40.1 us (98%)
  local copies, waits for them, and re-layouts  0.8 us (2%)
    pallas_call x1, Pallas kernels, local(): pl.pallas_call(kernel, out_shape=jax.ShapeDtypeStruct(split, f32), in_spe...  40.1 us

profile of v4, /device:TPU:17, one launch (start us, length us, event | category | flops | bytes accessed | tf_op | source)
XLA Modules:
  0.0 40.9 jit_solution(17647779495058675713)
XLA Ops:
  0.0 40.1 %shard_map.91 = f32[2,8,64,128]{3,2,1,0:T(8,128)S(1)} custom-call(f32[2,8,64,128]{3,2,1,0:T(8,128)} %bitcast.7, s32[16,64]{1,0:T(8,128)} %mask_hbm.1, f32[1,128]{1,0:T(1,128)} %bitcast.8, f32[1,128]{1,0:T(1,128)} %bitcast.9, bf16[128,512]{1,0:T(8,128)(2,1)} %w_proj_hbm.1, bf16[128,128]{1,0:T(8,128)(2,1)} %w_gate_hbm.1, f32[1,128]{1,0:T(1,128)} %bitcast.10, ...), custom_call_target="tpu_custom_call" | custom-call | tf_op jit(solution)/shard_map/pallas_call | solution.py:308
  40.1 0.8 %copy.11 = f32[16,64,128]{2,1,0:T(8,128)} copy(f32[16,64,128]{2,1,0:T(8,128)S(1)} %bitcast.6) | data formatting | bytes 1048576

commit v5 on v4

--- a/solution.py
+++ b/solution.py
@@ -199,29 +199,34 @@
 
         return store
 
-    def s_block(block, channels=range(HELD)):
-        tiles = []
-        for ch in channels:
-            r = jnp.concatenate([right[block * 4 + k, ch] for k in range(4)], axis=1)
-            s = dot(left[ch], jnp.concatenate([r, r], axis=0), NT)
-            tiles.append([
-                jnp.where(lane_low, s[16 * rr : 16 * rr + 8], s[16 * rr + 8 : 16 * rr + 16]) for rr in range(QUAD)
-            ])
-        first, count = channels[0] * 8, len(channels) * 8
-        dst = s_recv.at[pl.ds(pl.multiple_of(me * 32 + first, 8), count)]
-        for rr in range(QUAD):
-            tile = jnp.concatenate([t[rr] for t in tiles], axis=0)
-            mine = jnp.logical_and(block == col, quarter == rr)
-
-            @pl.when(mine)
-            def _():
-                dst[...] = tile
-
-            @pl.when(jnp.logical_not(mine))
-            def _():
+    def sums(*parts):
+        done = []
+        for block, channels in parts:
+            tiles = []
+            for ch in channels:
+                r = jnp.concatenate([right[block * 4 + k, ch] for k in range(4)], axis=1)
+                s = dot(left[ch], jnp.concatenate([r, r], axis=0), NT)
+                tiles.append([
+                    jnp.where(lane_low, s[16 * rr : 16 * rr + 8], s[16 * rr + 8 : 16 * rr + 16]) for rr in range(QUAD)
+                ])
+            done.append([jnp.concatenate([t[rr] for t in tiles], axis=0) for rr in range(QUAD)])
+        for (block, channels), tiles in zip(parts, done):
+            first, count = channels[0] * 8, len(channels) * 8
+            dst = s_recv.at[pl.ds(pl.multiple_of(me * 32 + first, 8), count)]
+            for rr in range(QUAD):
                 src = s_send.at[pl.ds(pl.multiple_of((block * QUAD + rr) * 32 + first, 8), count)]
-                src[...] = tile
-                move(src, dst, s_s, s_r, {"row": z * QUAD + rr, "col": block}).start()
+                src[...] = tiles[rr]
+            for rr in range(QUAD):
+                src = s_send.at[pl.ds(pl.multiple_of((block * QUAD + rr) * 32 + first, 8), count)]
+                mine = jnp.logical_and(block == col, quarter == rr)
+
+                @pl.when(mine)
+                def _():
+                    dst[...] = src[...]
+
+                @pl.when(jnp.logical_not(mine))
+                def _():
+                    move(src, dst, s_s, s_r, {"row": z * QUAD + rr, "col": block}).start()
 
     def forward(d):
         for e in range(4):
@@ -238,14 +243,14 @@
         for stream in streams:
             stream.half(n, 0).wait_recv()
             stream.half(n, 1).wait_recv()
-            s_block(stream.block(2), (stream.rest[n],))
+        sums(*((stream.block(2), (stream.rest[n],)) for stream in streams))
 
     def s_far(d):
-        for stream in streams:
-            s_block(stream.block(d), range(stream.far, stream.far + 2))
+        sums(*((stream.block(d), range(stream.far, stream.far + 2)) for stream in streams))
 
     forward(1)
     forward(2)
+    forward(3)
     arrived = recv_x.at[pl.ds(0, PEERS - 1)]
     move(arrived, arrived, send_x_sem, recv_x_sem, above).wait_recv()
     for k in range(4):
@@ -257,18 +262,16 @@
         regroup(recv_x, k, store_next)
     late(0, 0)
     late(0, 1)
+    late(1, 0)
     arrived = recv_l.at[pl.ds(0, PEERS - 1)]
     move(arrived, arrived, send_l_sem, recv_l_sem, above).wait_recv()
     for k in range(4):
         regroup(recv_l, k, store_left(k))
-    s_block(z)
-    forward(3)
-    late(1, 0)
-    for stream in streams:
-        s_block(stream.block(1))
-    s_far(2)
+    sums((z, range(HELD)))
+    sums(*((stream.block(1), range(HELD)) for stream in streams))
     forward(4)
     late(1, 1)
+    s_far(2)
     s_far(3)
     s_late(0)
     s_far(4)

time: 41 us -> 40.5 us (0.988)
  Pallas kernels: 40.1 us -> 39.6 us
    pallas_call x1, Pallas kernels: 40.1 us -> 39.6 us  [local(): pl.pallas_call(kernel, out_shape=jax.ShapeDtypeStruct(split, f32), in_spe...]
where the time goes in v5:
time: 40.5 us; the launch traced here: 40.4 us
  Pallas kernels  39.6 us (98%)
  local copies, waits for them, and re-layouts  0.8 us (2%)
    pallas_call x1, Pallas kernels, local(): pl.pallas_call(kernel, out_shape=jax.ShapeDtypeStruct(split, f32), in_spe...  39.6 us

profile of v5, /device:TPU:17, one launch (start us, length us, event | category | flops | bytes accessed | tf_op | source)
XLA Modules:
  0.0 40.4 jit_solution(4294019767879046430)
XLA Ops:
  0.0 39.6 %shard_map.91 = f32[2,8,64,128]{3,2,1,0:T(8,128)S(1)} custom-call(f32[2,8,64,128]{3,2,1,0:T(8,128)} %bitcast.7, s32[16,64]{1,0:T(8,128)} %mask_hbm.1, f32[1,128]{1,0:T(1,128)} %bitcast.8, f32[1,128]{1,0:T(1,128)} %bitcast.9, bf16[128,512]{1,0:T(8,128)(2,1)} %w_proj_hbm.1, bf16[128,128]{1,0:T(8,128)(2,1)} %w_gate_hbm.1, f32[1,128]{1,0:T(1,128)} %bitcast.10, ...), custom_call_target="tpu_custom_call" | custom-call | tf_op jit(solution)/shard_map/pallas_call | solution.py:311
  39.6 0.8 %copy.11 = f32[16,64,128]{2,1,0:T(8,128)} copy(f32[16,64,128]{2,1,0:T(8,128)S(1)} %bitcast.6) | data formatting | bytes 1048576

commit v6 on v5

--- a/solution.py
+++ b/solution.py
@@ -48,10 +48,18 @@
     def peer(other):
         return {"row": z * QUAD + lax.rem(other, QUAD), "col": lax.div(other, QUAD)}
 
+    at_x = [lax.rem(x + n, 4) for n in range(4)]
+    at_y = [lax.rem(y + n, 4) for n in range(4)]
+    at_core = [core, 1 - core]
+    pair_x, odd_x = [lax.div(v, 2) * 4 for v in at_x], [lax.rem(v, 2) * 2 for v in at_x]
+    row_x = [z * QUAD + v for v in odd_x]
+    slot_x = [4 * p + q for p, q in zip(pair_x, odd_x)]
+    slot_y = [4 * v for v in at_y]
+
     def each(reach, step):
         for dx, dy, dh in steps(reach):
-            to_x, to_y, to_core = lax.rem(x + dx, 4), lax.rem(y + dy, 4), lax.rem(core + dh, 2)
-            step(lax.div(to_x, 2) * 16 + to_y * 4 + lax.rem(to_x, 2) * 2 + to_core)
+            to = {"row": row_x[dx] + at_core[dh], "col": pair_x[dx] + at_y[dy]}
+            step(slot_x[dx] + slot_y[dy] + at_core[dh], to)
 
     x_in = pltpu.make_async_copy(x_hbm, x_ref, x_sem)
     small = [
@@ -64,7 +72,7 @@
     for copy in (*small[:4], x_in, *small[4:]):
         copy.start()
     barrier = pltpu.get_barrier_semaphore()
-    each(lambda hops: -hops, lambda o: pl.semaphore_signal(barrier, inc=1, device_id=peer(o), device_id_type=MESH))
+    each(lambda hops: -hops, lambda _, to: pl.semaphore_signal(barrier, inc=1, device_id=to, device_id_type=MESH))
     for neighbour in (above, below):
         pl.semaphore_signal(barrier, inc=1, device_id=neighbour, device_id_type=MESH)
 
@@ -122,21 +130,22 @@
         def raw(self, e):
             at = pl.ds(8 * near(e), 8)
             src, dst = send_r.at[at, self.rest[0] // 2], raw.at[at, self.far // 2]
-            return move(src, dst, self.sends, self.recvs.at[24 + e], self.to)
+            return move(src, dst, self.sends, self.recvs.at[17], self.to)
 
         def strip(self, d, e):
             part = right.at[self.block(d - 1) * 4 + near(e), pl.ds(self.far, 2)]
-            return move(part, part, self.sends, self.recvs.at[4 * (d - 1) + e], self.to)
+            return move(part, part, self.sends, self.recvs.at[4 * (d - 1) + e if d < 5 else 16], self.to)
 
         def half(self, n, h):
             part = right.at[pl.ds(self.block(1) * 4 + 2 * h, 2), self.rest[n]]
-            return move(part, part, self.sends, self.recvs.at[20 + 2 * n + h], self.to)
+            return move(part, part, self.sends, self.recvs.at[18 + n], self.to)
+
+        def wait(self, part, slot):
+            move(part, part, self.sends, self.recvs.at[slot], self.to).wait_recv()
 
     streams = (Stream(1, above, 0, up_s, up_r), Stream(-1, below, 2, down_s, down_r))
 
     def pass_on(e):
-        for stream in streams:
-            stream.raw(e).wait_recv()
         for n in range(0 if e else 1, 8):
             o = 8 * near(e) + lax.rem(me + n, 8)
             move(raw.at[o], recv_x.at[me], send_x_sem, recv_x_sem, peer(o)).start()
@@ -152,7 +161,7 @@
             stream.raw(e).start()
     each(
         lambda hops: (1, 2, 3, 4, 0)[hops],
-        lambda o: move(send_r.at[o], recv_r.at[me], send_r_sem, recv_r_sem.at[strip], peer(o)).start(),
+        lambda o, to: move(send_r.at[o], recv_r.at[me], send_r_sem, recv_r_sem.at[strip], to).start(),
     )
     recv_r[me] = send_r[me]
 
@@ -181,16 +190,16 @@
         regroup(recv_r, got, store_right)
         for stream in streams:
             stream.strip(1, e).start()
-        if e == 0:
-            pass_on(3)
-            pass_on(2)
+        if e == 1:
+            for stream in streams:
+                stream.wait(raw.at[pl.ds(0, 16)], 17)
+            for part in (3, 2, 1, 0):
+                pass_on(part)
+            recv_x[me] = raw[me]
         if e == 2:
-            pass_on(1)
-            pass_on(0)
-            recv_x[me] = raw[me]
             each(
                 lambda hops: -hops,
-                lambda o: move(send_l.at[o], recv_l.at[me], send_l_sem, recv_l_sem, peer(o)).start(),
+                lambda o, to: move(send_l.at[o], recv_l.at[me], send_l_sem, recv_l_sem, to).start(),
             )
 
     def store_left(strip):
@@ -228,12 +237,11 @@
                 def _():
                     move(src, dst, s_s, s_r, {"row": z * QUAD + rr, "col": block}).start()
 
-    def forward(d):
-        for e in range(4):
+    def forward(d, strips=range(4)):
+        for e in strips:
             for stream in streams:
                 stream.strip(d, e).wait_recv()
-                if d < 5:
-                    stream.strip(d + 1, e).start()
+                stream.strip(d + 1, e).start()
 
     def late(n, h):
         for stream in streams:
@@ -241,8 +249,7 @@
 
     def s_late(n):
         for stream in streams:
-            stream.half(n, 0).wait_recv()
-            stream.half(n, 1).wait_recv()
+            stream.wait(right.at[0], 18 + n)
         sums(*((stream.block(2), (stream.rest[n],)) for stream in streams))
 
     def s_far(d):
@@ -250,7 +257,7 @@
 
     forward(1)
     forward(2)
-    forward(3)
+    forward(3, range(1))
     arrived = recv_x.at[pl.ds(0, PEERS - 1)]
     move(arrived, arrived, send_x_sem, recv_x_sem, above).wait_recv()
     for k in range(4):
@@ -261,6 +268,7 @@
 
         regroup(recv_x, k, store_next)
     late(0, 0)
+    forward(3, range(1, 4))
     late(0, 1)
     late(1, 0)
     arrived = recv_l.at[pl.ds(0, PEERS - 1)]
@@ -275,7 +283,8 @@
     s_far(3)
     s_late(0)
     s_far(4)
-    forward(5)
+    for stream in streams:
+        stream.wait(right.at[pl.ds(0, 2)], 16)
     s_far(5)
     s_late(1)
 
@@ -330,7 +339,7 @@
             vmem((1024, 128), f32),
             vmem((1024, 128), f32),
             vmem((2, 128, 128), f32),
-            dma, dma((4,)), dma, dma, dma, dma, dma, dma((28,)), dma, dma((28,)), dma, dma,
+            dma, dma((4,)), dma, dma, dma, dma, dma, dma((20,)), dma, dma((20,)), dma, dma,
         ],
         compiler_params=pltpu.CompilerParams(
             collective_id=0, has_side_effects=True, vmem_limit_bytes=24 * 1024 * 1024

time: 40.5 us -> 40.2 us (level)
  no operation moved by 1% of the time
where the time goes in v6:
time: 40.2 us; the launch traced here: 40.1 us
  Pallas kernels  39.3 us (98%)
  local copies, waits for them, and re-layouts  0.8 us (2%)
    pallas_call x1, Pallas kernels, local(): pl.pallas_call(kernel, out_shape=jax.ShapeDtypeStruct(split, f32), in_spe...  39.3 us

profile of v6, /device:TPU:17, one launch (start us, length us, event | category | flops | bytes accessed | tf_op | source)
XLA Modules:
  0.0 40.1 jit_solution(1445838536128522483)
XLA Ops:
  0.0 39.3 %shard_map.91 = f32[2,8,64,128]{3,2,1,0:T(8,128)S(1)} custom-call(f32[2,8,64,128]{3,2,1,0:T(8,128)} %bitcast.7, s32[16,64]{1,0:T(8,128)} %mask_hbm.1, f32[1,128]{1,0:T(1,128)} %bitcast.8, f32[1,128]{1,0:T(1,128)} %bitcast.9, bf16[128,512]{1,0:T(8,128)(2,1)} %w_proj_hbm.1, bf16[128,128]{1,0:T(8,128)(2,1)} %w_gate_hbm.1, f32[1,128]{1,0:T(1,128)} %bitcast.10, ...), custom_call_target="tpu_custom_call" | custom-call | tf_op jit(solution)/shard_map/pallas_call | solution.py:320
  39.3 0.8 %copy.11 = f32[16,64,128]{2,1,0:T(8,128)} copy(f32[16,64,128]{2,1,0:T(8,128)S(1)} %bitcast.6) | data formatting | bytes 1048576

commit v7 on v6

--- a/solution.py
+++ b/solution.py
@@ -239,7 +239,7 @@
 
     def forward(d, strips=range(4)):
         for e in strips:
-            for stream in streams:
+            for stream in reversed(streams):
                 stream.strip(d, e).wait_recv()
                 stream.strip(d + 1, e).start()
 

time: 40.2 us -> 40 us (level)
  no operation moved by 1% of the time
where the time goes in v7:
time: 40 us; the launch traced here: 39.9 us
  Pallas kernels  39.1 us (98%)
  local copies, waits for them, and re-layouts  0.8 us (2%)
    pallas_call x1, Pallas kernels, local(): pl.pallas_call(kernel, out_shape=jax.ShapeDtypeStruct(split, f32), in_spe...  39.1 us

profile of v7, /device:TPU:17, one launch (start us, length us, event | category | flops | bytes accessed | tf_op | source)
XLA Modules:
  0.0 39.9 jit_solution(2617227004092976449)
XLA Ops:
  0.0 39.1 %shard_map.91 = f32[2,8,64,128]{3,2,1,0:T(8,128)S(1)} custom-call(f32[2,8,64,128]{3,2,1,0:T(8,128)} %bitcast.7, s32[16,64]{1,0:T(8,128)} %mask_hbm.1, f32[1,128]{1,0:T(1,128)} %bitcast.8, f32[1,128]{1,0:T(1,128)} %bitcast.9, bf16[128,512]{1,0:T(8,128)(2,1)} %w_proj_hbm.1, bf16[128,128]{1,0:T(8,128)(2,1)} %w_gate_hbm.1, f32[1,128]{1,0:T(1,128)} %bitcast.10, ...), custom_call_target="tpu_custom_call" | custom-call | tf_op jit(solution)/shard_map/pallas_call | solution.py:320
  39.1 0.8 %copy.11 = f32[16,64,128]{2,1,0:T(8,128)} copy(f32[16,64,128]{2,1,0:T(8,128)S(1)} %bitcast.6) | data formatting | bytes 1048576
